TPU v7x, 32 devices: a whole 2x2x4 slice. The times are simulated.
32 devices in a mesh: tm: 4 (over y, x), space: 8 (over z, core).
Axes of the slice: x: 2, y: 2, z: 4, core: 2. Of those that a mesh axis runs over, the one named last changes fastest.
Arguments:
- source: float32 [8, 1024, 5, 128], P('tm', 'space'), may hold values from -6 to 6
- terminal: float32 [1024, 5, 128], P('space'), may hold values from -6 to 6
- jacobian: float32 [4, 1024, 5, 5, 128], P('tm', 'space')
- face_coef: float32 [1024, 6, 128], P('space'), may hold values from 0.1 to 0.5
- cell_coef: float32 [1024, 128], P('space'), may hold values from 0.1 to 0.5
- neighbours: int32 [1024, 6], P('space'), may hold values from 0 to 160, as said below
- send_blocks: int32 [8, 2, 16], P('space'), may hold values from 0 to 127, as said below
- live_count: int32 [8], P('space'), may hold values from 64 to 128, as said below
- volume: float32 [1024, 128], P('space'), may hold values from 0.5 to 2
- shape_field: float32 [1024, 5, 128], P('space'), may hold values from -6 to 6
- weights: float32 [8], P('tm'), may hold values from 0.25 to 4
Outputs:
- adjoint: float32 [8, 1024, 5, 128], P('tm', 'space')
- sensitivity: float32 [1024], P('space')
Inputs may be any that keep to these rules, and one draw needn't show every extreme that they name: `live_count`: some device has 128 live blocks in every draw. `send_blocks`: each index names a live block of its own device. `neighbours`: a slot below 128 names a live block of the same device; 128 to 159 name received blocks, those of the lower device first; 160 is an empty slot.
All inputs are finite; a program needn't handle non-finite values.
Results may differ from a plain program's by a relative error of at most 0.00016.
Values sent between devices are 32-bit elements; how exact they have to be, the bound alone decides.
A program may use at most 64 MiB of HBM per device.

v0:
```python
import jax
import jax.numpy as jnp
from jax import lax
from jax.sharding import PartitionSpec as P

ITERS = 3


inverse_step = 6.0


def from_behind(value, axis, steps):
    count = lax.axis_size(axis)
    first, last = (max(0, -steps), min(count, count - steps))
    return lax.ppermute(value, axis, [(source, source + steps) for source in range(first, last)])


def pad_local(field):
    return jnp.pad(field, ((0, 0), (0, 0), (1, 1)))


def make_operator(face_coef, cell_coef, neighbours, mass, to_lower, to_higher, sides):
    highest = lax.Precision.HIGHEST
    along_coef = cell_coef[:, None, :]

    def operate(field, jac):
        from_lower = from_behind(field[to_higher], "space", 1)
        from_higher = from_behind(field[to_lower], "space", -1)
        blank = jnp.zeros((1,) + field.shape[1:], jnp.float32)
        extended = jnp.concatenate([field, from_lower, from_higher, blank], axis=0)
        gathered = extended[neighbours]
        coupled = jnp.einsum("bnc,bnkc->bkc", face_coef, gathered, precision=highest)
        own = jnp.einsum("bijc,bic->bjc", jac, field, precision=highest)
        widened = sides(field)
        beside = widened[:, :, :-2] + widened[:, :, 2:]
        return mass * field + own - coupled - along_coef * beside

    return operate


def make_precond(jac, mass, face_coef, cell_coef):
    diagonal = jnp.stack([jac[:, k, k, :] for k in range(jac.shape[1])], axis=1)
    return 1.0 / (
        mass + diagonal + jnp.sum(face_coef, axis=1)[:, None, :] + 2.0 * cell_coef[:, None, :]
    )


def sweep_levels(incoming, sources, jac, precond, mass, live, operate):

    def level_step(later, level_source):
        rhs = level_source + mass * later
        field = later
        for sweep in range(ITERS):
            field = live * (field + precond * (rhs - operate(field, jac)))
        return (field, field)

    return lax.scan(level_step, incoming, sources, reverse=True)


def per_device(
    source,
    terminal,
    jacobian,
    face_coef,
    cell_coef,
    neighbours,
    send_blocks,
    live_count,
    volume,
    shape_field,
    weights,
):
    nblocks = terminal.shape[0]
    live = (lax.iota(jnp.int32, nblocks) < live_count[0]).astype(jnp.float32)[:, None, None]
    mass = (inverse_step * volume)[:, None, :]
    to_lower = send_blocks[0, 0]
    to_higher = send_blocks[0, 1]
    rounds = lax.axis_size("tm")
    jac = jacobian[0]
    precond = make_precond(jac, mass, face_coef, cell_coef)
    operate = make_operator(face_coef, cell_coef, neighbours, mass, to_lower, to_higher, pad_local)

    def slab(incoming):
        return sweep_levels(incoming, source, jac, precond, mass, live, operate)

    is_last = lax.axis_index("tm") == rounds - 1
    start = live * terminal

    def turn(step_index, incoming):
        first, fields = slab(incoming)
        moved = from_behind(first, "tm", -1)
        return jnp.where(is_last, start, moved)

    incoming = lax.fori_loop(0, rounds - 1, turn, start)
    first, fields = slab(incoming)
    sensitivity = lax.psum(
        jnp.sum(weights[:, None] * jnp.sum(fields * shape_field[None], axis=(2, 3)), axis=0), "tm"
    )
    return (fields, sensitivity)


def solution(mesh):
    return jax.shard_map(
        per_device,
        mesh=mesh,
        in_specs=(
            P("tm", "space", None, None),
            P("space", None, None),
            P("tm", "space", None, None, None),
            P("space", None, None),
            P("space", None),
            P("space", None),
            P("space", None, None),
            P("space"),
            P("space", None),
            P("space", None, None),
            P("tm"),
        ),
        out_specs=(P("tm", "space", None, None), P("space")),
        check_vma=False,
    )
```

profile of v0, /device:TPU:1, one launch (start us, length us, event | category | flops | bytes accessed | tf_op | source)
XLA Modules:
  0.0 558.8 jit_solution(6534737591268335306)
XLA Ops:
  11.9 403.6 %while.60 = (s32[]{:T(128)}, f32[128,5,128]{2,1,0:T(8,128)S(1)}, pred[]{:T(512)}, f32[2,128,5,128]{3,2,1,0:T(8,128)}, f32[128,1,128]{2,0,1:T(8,128)S(1)}, /*inde...) while((s32[]{:T(128)}, f32[128,5,128]{2,1,0:T(8,128)S(1)}, ...), condition=%wide.region_4.5_spmd.clone, body=%wide.region_1.4_spmd.clone.sunk | while | flops 8797413 | bytes 66983056 | solution.py:94
  13.1 117.6 %while.62 = (s32[]{:T(128)}, f32[128,5,128]{2,1,0:T(8,128)S(1)}, f32[128,1,1]{0,2,1:T(1,128)}, f32[2,128,5,128]{3,2,1,0:T(8,128)}, f32[128,1,128]{2,0,1:T(8,128)...) while((s32[]{:T(128)}, f32[128,5,128]{2,1,0:T(8,128)S(1)}, ...), condition=%wide.region_3.3_spmd, body=%wide.region_2.2_spmd.sunk | while | flops 8715235 | bytes 64688432 | solution.py:57
  16.9 4.6 collective-permute-start.7
  26.5 3.6 gather_fusion.11
  76.3 3.6 collective-permute-start.7
  132.0 13.0 %collective-permute-done.12 = f32[128,5,128]{2,1,0:T(8,128)} collective-permute-done((f32[128,5,128]{2,1,0:T(8,128)S(1)}, f32[128,5,128]{2,1,0:T(8,128)}, u32[]{:S(2)}, u32[]{:S(2)}) %collective-permute-start.12) | collective-permute-done | bytes 327712 | tf_op jit(solution)/shard_map/while/body/eval_jaxpr/ppermute | solution.py:15
  147.2 117.6 %while.62 = (s32[]{:T(128)}, f32[128,5,128]{2,1,0:T(8,128)S(1)}, f32[128,1,1]{0,2,1:T(1,128)}, f32[2,128,5,128]{3,2,1,0:T(8,128)}, f32[128,1,128]{2,0,1:T(8,128)...) while((s32[]{:T(128)}, f32[128,5,128]{2,1,0:T(8,128)S(1)}, ...), condition=%wide.region_3.3_spmd, body=%wide.region_2.2_spmd.sunk | while | flops 8715235 | bytes 64688432 | solution.py:57
  151.0 4.6 collective-permute-start.7
  210.4 3.6 collective-permute-start.7
  266.1 13.3 %collective-permute-done.12 = f32[128,5,128]{2,1,0:T(8,128)} collective-permute-done((f32[128,5,128]{2,1,0:T(8,128)S(1)}, f32[128,5,128]{2,1,0:T(8,128)}, u32[]{:S(2)}, u32[]{:S(2)}) %collective-permute-start.12) | collective-permute-done | bytes 327712 | tf_op jit(solution)/shard_map/while/body/eval_jaxpr/ppermute | solution.py:15
  281.7 117.3 %while.62 = (s32[]{:T(128)}, f32[128,5,128]{2,1,0:T(8,128)S(1)}, f32[128,1,1]{0,2,1:T(1,128)}, f32[2,128,5,128]{3,2,1,0:T(8,128)}, f32[128,1,128]{2,0,1:T(8,128)...) while((s32[]{:T(128)}, f32[128,5,128]{2,1,0:T(8,128)S(1)}, ...), condition=%wide.region_3.3_spmd, body=%wide.region_2.2_spmd.sunk | while | flops 8715235 | bytes 64688432 | solution.py:57
  285.5 4.3 collective-permute-start.7
  344.6 3.6 collective-permute-start.7
  400.3 14.1 %collective-permute-done.12 = f32[128,5,128]{2,1,0:T(8,128)} collective-permute-done((f32[128,5,128]{2,1,0:T(8,128)S(1)}, f32[128,5,128]{2,1,0:T(8,128)}, u32[]{:S(2)}, u32[]{:S(2)}) %collective-permute-start.12) | collective-permute-done | bytes 327712 | tf_op jit(solution)/shard_map/while/body/eval_jaxpr/ppermute | solution.py:15
  416.7 128.5 %while.61 = (s32[]{:T(128)}, f32[128,5,128]{2,1,0:T(8,128)S(1)}, f32[2,128,5,128]{3,2,1,0:T(8,128)}, f32[2,128,5,128]{3,2,1,0:T(8,128)}, f32[128,1,128]{2,0,1:T(...) while((s32[]{:T(128)}, f32[128,5,128]{2,1,0:T(8,128)S(1)}, ...), condition=%wide.region_6.7_spmd.clone, body=%wide.region_5.6_spmd.clone.sunk | while | flops 8715491 | bytes 66577184 | solution.py:57
  421.0 4.2 collective-permute-start.1
  430.7 3.9 gather_fusion.2
  451.8 3.9 gather_fusion.5
  472.8 3.9 gather_fusion.8
  485.7 3.6 collective-permute-start.1
  494.8 3.9 gather_fusion.2
  515.5 3.9 gather_fusion.5
  536.6 3.9 gather_fusion.8
  549.7 9.1 %psum.7 = f32[128]{0:T(128)} all-reduce(f32[128]{0:T(128)S(1)} %multiply_reduce_fusion.13), channel_id=1, replica_groups=mesh['tm'=4,'space'=8] {'tm'}, use_global_device_ids=true, to_apply=%region_9.10 | all-reduce | flops 128 | bytes 1024 | tf_op jit(solution)/shard_map/psum | solution.py:96
  (727 shorter events, 445.5 us)
Async XLA Ops:
  13.7 11.4 %collective-permute-start.6 = (f32[16,5,128]{2,1,0:T(8,128)S(1)}, f32[16,5,128]{2,1,0:T(8,128)S(1)}, u32[]{:S(2)}, u32[]{:S(2)}) collective-permute-start(f32[16,5,128]{2,1,0:T(8,128)S(1)} %gather_fusion.9), channel_id=1, source_target_pairs={{1,0},{2,1},{3,2},{4,3},{5,4},{6,5},{7,6},{9,8},{10,9},{11,10},{12... | collective-permute-start | bytes 122888 | tf_op jit(solution)/shard_map/while/body/eval_jaxpr/while/body/eval_jaxpr/ppermute | solution.py:15
  16.9 8.3 %collective-permute-start.7 = (f32[16,5,128]{2,1,0:T(8,128)}, f32[16,5,128]{2,1,0:T(8,128)}, u32[]{:S(2)}, u32[]{:S(2)}) collective-permute-start(f32[16,5,128]{2,1,0:T(8,128)} %gather_fusion.10), channel_id=1, source_target_pairs={{0,1},{1,2},{2,3},{3,4},{4,5},{5,6},{6,7},{8,9},{9,10},{10,11},{11... | collective-permute-start | bytes 122888 | tf_op jit(solution)/shard_map/while/body/eval_jaxpr/while/body/eval_jaxpr/ppermute | solution.py:15
  37.6 6.8 %collective-permute-start.9 = (f32[16,5,128]{2,1,0:T(8,128)S(1)}, f32[16,5,128]{2,1,0:T(8,128)S(1)}, u32[]{:S(2)}, u32[]{:S(2)}) collective-permute-start(f32[16,5,128]{2,1,0:T(8,128)S(1)} %gather_fusion.13), channel_id=1, source_target_pairs={{0,1},{1,2},{2,3},{3,4},{4,5},{5,6},{6,7},{8,9},{9,10},{10,11},{11... | collective-permute-start | bytes 122888 | tf_op jit(solution)/shard_map/while/body/eval_jaxpr/while/body/eval_jaxpr/ppermute | solution.py:15
  57.1 6.8 %collective-permute-start.11 = (f32[16,5,128]{2,1,0:T(8,128)S(1)}, f32[16,5,128]{2,1,0:T(8,128)S(1)}, u32[]{:S(2)}, u32[]{:S(2)}) collective-permute-start(f32[16,5,128]{2,1,0:T(8,128)S(1)} %gather_fusion.16), channel_id=1, source_target_pairs={{0,1},{1,2},{2,3},{3,4},{4,5},{5,6},{6,7},{8,9},{9,10},{10,11},{11... | collective-permute-start | bytes 122888 | tf_op jit(solution)/shard_map/while/body/eval_jaxpr/while/body/eval_jaxpr/ppermute | solution.py:15
  73.1 10.5 %collective-permute-start.6 = (f32[16,5,128]{2,1,0:T(8,128)S(1)}, f32[16,5,128]{2,1,0:T(8,128)S(1)}, u32[]{:S(2)}, u32[]{:S(2)}) collective-permute-start(f32[16,5,128]{2,1,0:T(8,128)S(1)} %gather_fusion.9), channel_id=1, source_target_pairs={{1,0},{2,1},{3,2},{4,3},{5,4},{6,5},{7,6},{9,8},{10,9},{11,10},{12... | collective-permute-start | bytes 122888 | tf_op jit(solution)/shard_map/while/body/eval_jaxpr/while/body/eval_jaxpr/ppermute | solution.py:15
  76.3 7.3 %collective-permute-start.7 = (f32[16,5,128]{2,1,0:T(8,128)}, f32[16,5,128]{2,1,0:T(8,128)}, u32[]{:S(2)}, u32[]{:S(2)}) collective-permute-start(f32[16,5,128]{2,1,0:T(8,128)} %gather_fusion.10), channel_id=1, source_target_pairs={{0,1},{1,2},{2,3},{3,4},{4,5},{5,6},{6,7},{8,9},{9,10},{10,11},{11... | collective-permute-start | bytes 122888 | tf_op jit(solution)/shard_map/while/body/eval_jaxpr/while/body/eval_jaxpr/ppermute | solution.py:15
  96.0 6.8 %collective-permute-start.9 = (f32[16,5,128]{2,1,0:T(8,128)S(1)}, f32[16,5,128]{2,1,0:T(8,128)S(1)}, u32[]{:S(2)}, u32[]{:S(2)}) collective-permute-start(f32[16,5,128]{2,1,0:T(8,128)S(1)} %gather_fusion.13), channel_id=1, source_target_pairs={{0,1},{1,2},{2,3},{3,4},{4,5},{5,6},{6,7},{8,9},{9,10},{10,11},{11... | collective-permute-start | bytes 122888 | tf_op jit(solution)/shard_map/while/body/eval_jaxpr/while/body/eval_jaxpr/ppermute | solution.py:15
  130.7 14.3 %collective-permute-start.12 = (f32[128,5,128]{2,1,0:T(8,128)S(1)}, f32[128,5,128]{2,1,0:T(8,128)}, u32[]{:S(2)}, u32[]{:S(2)}) collective-permute-start(f32[128,5,128]{2,1,0:T(8,128)S(1)} %get-tuple-element.1285), channel_id=1, source_target_pairs={{8,0},{16,8},{24,16},{9,1},{17,9},{25,17},{10,2},{18,10},{26,18},{... | collective-permute-start | bytes 983048 | tf_op jit(solution)/shard_map/while/body/eval_jaxpr/ppermute | solution.py:15
  147.8 11.4 %collective-permute-start.6 = (f32[16,5,128]{2,1,0:T(8,128)S(1)}, f32[16,5,128]{2,1,0:T(8,128)S(1)}, u32[]{:S(2)}, u32[]{:S(2)}) collective-permute-start(f32[16,5,128]{2,1,0:T(8,128)S(1)} %gather_fusion.9), channel_id=1, source_target_pairs={{1,0},{2,1},{3,2},{4,3},{5,4},{6,5},{7,6},{9,8},{10,9},{11,10},{12... | collective-permute-start | bytes 122888 | tf_op jit(solution)/shard_map/while/body/eval_jaxpr/while/body/eval_jaxpr/ppermute | solution.py:15
  151.0 8.3 %collective-permute-start.7 = (f32[16,5,128]{2,1,0:T(8,128)}, f32[16,5,128]{2,1,0:T(8,128)}, u32[]{:S(2)}, u32[]{:S(2)}) collective-permute-start(f32[16,5,128]{2,1,0:T(8,128)} %gather_fusion.10), channel_id=1, source_target_pairs={{0,1},{1,2},{2,3},{3,4},{4,5},{5,6},{6,7},{8,9},{9,10},{10,11},{11... | collective-permute-start | bytes 122888 | tf_op jit(solution)/shard_map/while/body/eval_jaxpr/while/body/eval_jaxpr/ppermute | solution.py:15
  171.7 6.8 %collective-permute-start.9 = (f32[16,5,128]{2,1,0:T(8,128)S(1)}, f32[16,5,128]{2,1,0:T(8,128)S(1)}, u32[]{:S(2)}, u32[]{:S(2)}) collective-permute-start(f32[16,5,128]{2,1,0:T(8,128)S(1)} %gather_fusion.13), channel_id=1, source_target_pairs={{0,1},{1,2},{2,3},{3,4},{4,5},{5,6},{6,7},{8,9},{9,10},{10,11},{11... | collective-permute-start | bytes 122888 | tf_op jit(solution)/shard_map/while/body/eval_jaxpr/while/body/eval_jaxpr/ppermute | solution.py:15
  207.2 10.5 %collective-permute-start.6 = (f32[16,5,128]{2,1,0:T(8,128)S(1)}, f32[16,5,128]{2,1,0:T(8,128)S(1)}, u32[]{:S(2)}, u32[]{:S(2)}) collective-permute-start(f32[16,5,128]{2,1,0:T(8,128)S(1)} %gather_fusion.9), channel_id=1, source_target_pairs={{1,0},{2,1},{3,2},{4,3},{5,4},{6,5},{7,6},{9,8},{10,9},{11,10},{12... | collective-permute-start | bytes 122888 | tf_op jit(solution)/shard_map/while/body/eval_jaxpr/while/body/eval_jaxpr/ppermute | solution.py:15
  210.4 7.3 %collective-permute-start.7 = (f32[16,5,128]{2,1,0:T(8,128)}, f32[16,5,128]{2,1,0:T(8,128)}, u32[]{:S(2)}, u32[]{:S(2)}) collective-permute-start(f32[16,5,128]{2,1,0:T(8,128)} %gather_fusion.10), channel_id=1, source_target_pairs={{0,1},{1,2},{2,3},{3,4},{4,5},{5,6},{6,7},{8,9},{9,10},{10,11},{11... | collective-permute-start | bytes 122888 | tf_op jit(solution)/shard_map/while/body/eval_jaxpr/while/body/eval_jaxpr/ppermute | solution.py:15
  264.8 14.6 %collective-permute-start.12 = (f32[128,5,128]{2,1,0:T(8,128)S(1)}, f32[128,5,128]{2,1,0:T(8,128)}, u32[]{:S(2)}, u32[]{:S(2)}) collective-permute-start(f32[128,5,128]{2,1,0:T(8,128)S(1)} %get-tuple-element.1285), channel_id=1, source_target_pairs={{8,0},{16,8},{24,16},{9,1},{17,9},{25,17},{10,2},{18,10},{26,18},{... | collective-permute-start | bytes 983048 | tf_op jit(solution)/shard_map/while/body/eval_jaxpr/ppermute | solution.py:15
  282.3 11.1 %collective-permute-start.6 = (f32[16,5,128]{2,1,0:T(8,128)S(1)}, f32[16,5,128]{2,1,0:T(8,128)S(1)}, u32[]{:S(2)}, u32[]{:S(2)}) collective-permute-start(f32[16,5,128]{2,1,0:T(8,128)S(1)} %gather_fusion.9), channel_id=1, source_target_pairs={{1,0},{2,1},{3,2},{4,3},{5,4},{6,5},{7,6},{9,8},{10,9},{11,10},{12... | collective-permute-start | bytes 122888 | tf_op jit(solution)/shard_map/while/body/eval_jaxpr/while/body/eval_jaxpr/ppermute | solution.py:15
  285.5 8.0 %collective-permute-start.7 = (f32[16,5,128]{2,1,0:T(8,128)}, f32[16,5,128]{2,1,0:T(8,128)}, u32[]{:S(2)}, u32[]{:S(2)}) collective-permute-start(f32[16,5,128]{2,1,0:T(8,128)} %gather_fusion.10), channel_id=1, source_target_pairs={{0,1},{1,2},{2,3},{3,4},{4,5},{5,6},{6,7},{8,9},{9,10},{10,11},{11... | collective-permute-start | bytes 122888 | tf_op jit(solution)/shard_map/while/body/eval_jaxpr/while/body/eval_jaxpr/ppermute | solution.py:15
  305.9 6.8 %collective-permute-start.9 = (f32[16,5,128]{2,1,0:T(8,128)S(1)}, f32[16,5,128]{2,1,0:T(8,128)S(1)}, u32[]{:S(2)}, u32[]{:S(2)}) collective-permute-start(f32[16,5,128]{2,1,0:T(8,128)S(1)} %gather_fusion.13), channel_id=1, source_target_pairs={{0,1},{1,2},{2,3},{3,4},{4,5},{5,6},{6,7},{8,9},{9,10},{10,11},{11... | collective-permute-start | bytes 122888 | tf_op jit(solution)/shard_map/while/body/eval_jaxpr/while/body/eval_jaxpr/ppermute | solution.py:15
  341.4 10.5 %collective-permute-start.6 = (f32[16,5,128]{2,1,0:T(8,128)S(1)}, f32[16,5,128]{2,1,0:T(8,128)S(1)}, u32[]{:S(2)}, u32[]{:S(2)}) collective-permute-start(f32[16,5,128]{2,1,0:T(8,128)S(1)} %gather_fusion.9), channel_id=1, source_target_pairs={{1,0},{2,1},{3,2},{4,3},{5,4},{6,5},{7,6},{9,8},{10,9},{11,10},{12... | collective-permute-start | bytes 122888 | tf_op jit(solution)/shard_map/while/body/eval_jaxpr/while/body/eval_jaxpr/ppermute | solution.py:15
  344.6 7.3 %collective-permute-start.7 = (f32[16,5,128]{2,1,0:T(8,128)}, f32[16,5,128]{2,1,0:T(8,128)}, u32[]{:S(2)}, u32[]{:S(2)}) collective-permute-start(f32[16,5,128]{2,1,0:T(8,128)} %gather_fusion.10), channel_id=1, source_target_pairs={{0,1},{1,2},{2,3},{3,4},{4,5},{5,6},{6,7},{8,9},{9,10},{10,11},{11... | collective-permute-start | bytes 122888 | tf_op jit(solution)/shard_map/while/body/eval_jaxpr/while/body/eval_jaxpr/ppermute | solution.py:15
  399.0 15.4 %collective-permute-start.12 = (f32[128,5,128]{2,1,0:T(8,128)S(1)}, f32[128,5,128]{2,1,0:T(8,128)}, u32[]{:S(2)}, u32[]{:S(2)}) collective-permute-start(f32[128,5,128]{2,1,0:T(8,128)S(1)} %get-tuple-element.1285), channel_id=1, source_target_pairs={{8,0},{16,8},{24,16},{9,1},{17,9},{25,17},{10,2},{18,10},{26,18},{... | collective-permute-start | bytes 983048 | tf_op jit(solution)/shard_map/while/body/eval_jaxpr/ppermute | solution.py:15
  417.9 11.7 %collective-permute-start = (f32[16,5,128]{2,1,0:T(8,128)}, f32[16,5,128]{2,1,0:T(8,128)S(1)}, u32[]{:S(2)}, u32[]{:S(2)}) collective-permute-start(f32[16,5,128]{2,1,0:T(8,128)} %gather_fusion), channel_id=1, source_target_pairs={{1,0},{2,1},{3,2},{4,3},{5,4},{6,5},{7,6},{9,8},{10,9},{11,10},{12... | collective-permute-start | bytes 122888 | tf_op jit(solution)/shard_map/while/body/eval_jaxpr/ppermute | solution.py:15
  421.0 8.6 %collective-permute-start.1 = (f32[16,5,128]{2,1,0:T(8,128)}, f32[16,5,128]{2,1,0:T(8,128)S(1)}, u32[]{:S(2)}, u32[]{:S(2)}) collective-permute-start(f32[16,5,128]{2,1,0:T(8,128)} %gather_fusion.1), channel_id=1, source_target_pairs={{0,1},{1,2},{2,3},{3,4},{4,5},{5,6},{6,7},{8,9},{9,10},{10,11},{11... | collective-permute-start | bytes 122888 | tf_op jit(solution)/shard_map/while/body/eval_jaxpr/ppermute | solution.py:15
  482.6 11.1 %collective-permute-start = (f32[16,5,128]{2,1,0:T(8,128)}, f32[16,5,128]{2,1,0:T(8,128)S(1)}, u32[]{:S(2)}, u32[]{:S(2)}) collective-permute-start(f32[16,5,128]{2,1,0:T(8,128)} %gather_fusion), channel_id=1, source_target_pairs={{1,0},{2,1},{3,2},{4,3},{5,4},{6,5},{7,6},{9,8},{10,9},{11,10},{12... | collective-permute-start | bytes 122888 | tf_op jit(solution)/shard_map/while/body/eval_jaxpr/ppermute | solution.py:15
  485.7 8.0 %collective-permute-start.1 = (f32[16,5,128]{2,1,0:T(8,128)}, f32[16,5,128]{2,1,0:T(8,128)S(1)}, u32[]{:S(2)}, u32[]{:S(2)}) collective-permute-start(f32[16,5,128]{2,1,0:T(8,128)} %gather_fusion.1), channel_id=1, source_target_pairs={{0,1},{1,2},{2,3},{3,4},{4,5},{5,6},{6,7},{8,9},{9,10},{10,11},{11... | collective-permute-start | bytes 122888 | tf_op jit(solution)/shard_map/while/body/eval_jaxpr/ppermute | solution.py:15
  (216 other events, 990.2 us)
where the time goes:
time: 564 us; the launch traced here: 559 us
  local copies, waits for them, and re-layouts  192 us (34%)
  other arithmetic  170 us (30%)
  starting transfers between devices  123 us (22%)
  waiting for transfers between devices  60 us (11%)
  blocking collectives  9.11 us (2%)
    ppermute x51, starting transfers between devices, from_behind(): lax.ppermute(value, axis, [(source, source + steps) for source in range(f...  123 us
    gather x24, local copies, waits for them, and re-layouts, operate(): gathered = extended[neighbours]  88 us
    dot_general x24, other arithmetic, operate(): jnp.einsum('bnc,bnkc->bkc', face_coef, gathered, precision=highest)  66.7 us
    ppermute x51, waiting for transfers between devices, from_behind(): lax.ppermute(value, axis, [(source, source + steps) for source in range(f...  60 us
    dot_general x24, other arithmetic, operate(): own = jnp.einsum('bijc,bic->bjc', jac, field, precision=highest)  48.4 us
    gather x24, local copies, waits for them, and re-layouts, operate(): from_lower = from_behind(field[to_higher], 'space', 1)  39 us
    gather x24, local copies, waits for them, and re-layouts, operate(): from_higher = from_behind(field[to_lower], 'space', -1)  31.3 us
    mul x24, other arithmetic, level_step(): field = live * (field + precond * (rhs - operate(field, jac)))  25.3 us
  transfers between devices with their start and end apart: 51, of which 19 were waited for; matrix products, arithmetic and copies ran while one was open for 14% of the time, Pallas kernels for 0%

commit v1 on v0

v1 whole, which is shorter than its diff:
```python
import functools

import jax
import jax.numpy as jnp
from jax import lax
from jax.experimental import pallas as pl
from jax.experimental.pallas import tpu as pltpu
from jax.sharding import PartitionSpec as P

ITERS = 3
INVERSE_STEP = 6.0
UNROLL = 8


def kernel(
    groups,
    width,
    source_hbm,
    terminal_hbm,
    jac_hbm,
    face_hbm,
    cell_hbm,
    nbr,
    send_blocks,
    live_count,
    volume_hbm,
    shape_hbm,
    weights,
    adjoint_hbm,
    sens_ref,
    source,
    terminal,
    jac,
    face,
    cell,
    volume,
    shape,
    field,
    part,
    rate,
    rate_cell,
    rate_mass,
    rhs,
    levels,
    weighted,
    halo,
    edge,
    outbox,
    acc_in,
    acc_out,
    total,
    load_sem,
    store_sem,
    halo_send,
    halo_recv,
    state_send,
    state_recv,
    acc_send,
    acc_recv,
    total_send,
    total_recv,
):
    g = lax.axis_index("tm")
    d = lax.axis_index("space")
    steps, nb, comp, cells = source.shape
    nei = face.shape[1]
    count = outbox.shape[2]
    sweeps = steps * ITERS

    loads = [
        pltpu.make_async_copy(jac_hbm.at[0], jac, load_sem.at[0]),
        pltpu.make_async_copy(face_hbm, face, load_sem.at[1]),
        pltpu.make_async_copy(cell_hbm, cell, load_sem.at[2]),
        pltpu.make_async_copy(volume_hbm, volume, load_sem.at[3]),
        pltpu.make_async_copy(terminal_hbm, terminal, load_sem.at[4]),
        pltpu.make_async_copy(source_hbm, source, load_sem.at[5]),
        pltpu.make_async_copy(shape_hbm, shape, load_sem.at[6]),
    ]
    for load in loads:
        load.start()

    zero = jnp.zeros((comp, cells), jnp.float32)
    field[nb] = zero

    def clear(m, _):
        for row in range(halo.shape[1]):
            halo[m, row] = zero
        return 0

    edge[0] = zero
    edge[2 * count + 1] = zero

    lax.fori_loop(0, sweeps, clear, 0)

    barrier = pltpu.get_barrier_semaphore()
    for other in range(groups):
        @pl.when(g != other)
        def _():
            pl.semaphore_signal(barrier, inc=1, device_id={"tm": other})

    @pl.when(d > 0)
    def _():
        pl.semaphore_signal(barrier, inc=1, device_id={"space": d - 1})

    @pl.when(d < width - 1)
    def _():
        pl.semaphore_signal(barrier, inc=1, device_id={"space": d + 1})

    pl.semaphore_wait(
        barrier,
        groups - 1 + jnp.where(d > 0, 1, 0) + jnp.where(d < width - 1, 1, 0),
    )
    for load in loads:
        load.wait()

    row_id = lax.broadcasted_iota(jnp.int32, (comp, cells), 0)
    lane_id = lax.broadcasted_iota(jnp.int32, (comp, cells), 1)
    alive = live_count[0]

    def prepare(b, _):
        live = jnp.where(b < alive, 1.0, 0.0)
        mass = INVERSE_STEP * volume[pl.ds(b, 1), :]
        along = cell[pl.ds(b, 1), :]
        base = mass + jnp.sum(face[b], axis=0, keepdims=True) + 2.0 * along
        diagonal = jnp.broadcast_to(base, (comp, cells))
        for i in range(comp):
            diagonal = diagonal + jnp.where(row_id == i, jac[b, i], 0.0)
        c = live / diagonal
        rate[b] = c
        rate_cell[b] = c * along
        drift = c * mass
        rate_mass[b] = drift
        for i in range(comp):
            jac[b, i] = jnp.where(row_id == i, live - drift, 0.0) - c * jac[b, i]
        weighted[b] = zero
        return 0

    lax.fori_loop(0, nb, prepare, 0, unroll=4)

    def state_copy(to):
        return pltpu.make_async_remote_copy(
            src_ref=field.at[pl.ds(0, nb)],
            dst_ref=field.at[pl.ds(0, nb)],
            send_sem=state_send,
            recv_sem=state_recv,
            device_id={"tm": to},
        )

    @pl.when(g == groups - 1)
    def _():
        def begin(b, _):
            field[b] = jnp.where(b < alive, 1.0, 0.0) * terminal[b]
            return 0

        lax.fori_loop(0, nb, begin, 0, unroll=8)

    @pl.when(g < groups - 1)
    def _():
        state_copy(g).wait_recv()

    def halo_copy(m, side, to):
        return pltpu.make_async_remote_copy(
            src_ref=outbox.at[m, side],
            dst_ref=halo.at[m, pl.ds((1 - side) * count, count)],
            send_sem=halo_send.at[m, side],
            recv_sem=halo_recv.at[m, 1 - side],
            device_id={"space": to},
        )

    def send(m):
        @pl.when(d > 0)
        def _():
            halo_copy(m, 0, d - 1).start()

        @pl.when(d < width - 1)
        def _():
            halo_copy(m, 1, d + 1).start()

    def receive(m):
        @pl.when(d > 0)
        def _():
            halo_copy(m, 1, d - 1).wait_recv()

        @pl.when(d < width - 1)
        def _():
            halo_copy(m, 0, d + 1).wait_recv()

    def remote(b):
        value = None
        for k in range(nei):
            slot = jnp.maximum(nbr[b, k], nb - 1) - (nb - 1)
            term = face[b, pl.ds(k, 1), :] * edge[slot]
            value = term if value is None else value + term
        return part[b] + rate[b] * value

    for side in range(2):
        for s in range(count):
            outbox[0, side, s] = field[send_blocks[0, side, s]]
    send(0)

    def sweep(m, n):
        def local(b0, _):
            for u in range(UNROLL):
                b = b0 * UNROLL + u
                x = field[b]
                left = jnp.where(lane_id == 0, 0.0, pltpu.roll(x, 1, 1))
                right = jnp.where(lane_id == cells - 1, 0.0, pltpu.roll(x, cells - 1, 1))
                value = rhs[b] + rate_cell[b] * (left + right)
                for i in range(comp):
                    value = value + jac[b, i] * field[b, pl.ds(i, 1), :]
                near = None
                for k in range(nei):
                    term = face[b, pl.ds(k, 1), :] * field[jnp.minimum(nbr[b, k], nb)]
                    near = term if near is None else near + term
                part[b] = value + rate[b] * near
            return 0

        lax.fori_loop(0, nb // UNROLL, local, 0)
        receive(m)
        for row in range(2 * count):
            edge[1 + row] = halo[m, row]

        @pl.when(m + 1 < sweeps)
        def _():
            for side in range(2):
                for s in range(count):
                    outbox[m + 1, side, s] = remote(send_blocks[0, side, s])
            send(m + 1)

        def bulk(b0, _):
            for u in range(UNROLL):
                b = b0 * UNROLL + u
                field[b] = remote(b)
            return 0

        lax.fori_loop(0, nb // UNROLL, bulk, 0)

    def level_copy(n):
        return pltpu.make_async_copy(levels.at[n], adjoint_hbm.at[n], store_sem.at[n])

    def level(t, _):
        n = steps - 1 - t

        def start(b0, _):
            for u in range(UNROLL):
                b = b0 * UNROLL + u
                rhs[b] = rate[b] * source[n, b] + rate_mass[b] * field[b]
            return 0

        lax.fori_loop(0, nb // UNROLL, start, 0)

        def inner(it, _):
            sweep(t * ITERS + it, n)
            return 0

        lax.fori_loop(0, ITERS, inner, 0)

        @pl.when((t == steps - 1) & (g > 0))
        def _():
            state_copy(g - 1).start()

        weight = weights[n]

        def finish(b0, _):
            for u in range(UNROLL):
                b = b0 * UNROLL + u
                x = field[b]
                levels[n, b] = x
                weighted[b] = weighted[b] + weight * x
            return 0

        lax.fori_loop(0, nb // UNROLL, finish, 0)
        level_copy(n).start()
        return 0

    lax.fori_loop(0, steps, level, 0)

    summed = jnp.sum(weighted[...] * shape[...], axis=1)
    mine = lax.dot_general(
        jnp.ones((8, cells), jnp.float32),
        summed,
        (((1,), (1,)), ((), ())),
        precision=lax.Precision.HIGHEST,
        preferred_element_type=jnp.float32,
    )

    def acc_copy(to):
        return pltpu.make_async_remote_copy(
            src_ref=acc_out, dst_ref=acc_in, send_sem=acc_send, recv_sem=acc_recv,
            device_id={"tm": to},
        )

    def total_copy(to):
        return pltpu.make_async_remote_copy(
            src_ref=acc_out, dst_ref=total, send_sem=total_send.at[to], recv_sem=total_recv,
            device_id={"tm": to},
        )

    @pl.when(g == groups - 1)
    def _():
        acc_out[...] = mine

    @pl.when(g < groups - 1)
    def _():
        acc_copy(g).wait_recv()
        acc_out[...] = mine + acc_in[...]

    @pl.when(g > 0)
    def _():
        acc_copy(g - 1).start()
        total_copy(g).wait_recv()
        sens_ref[...] = total[0:1, :]

    @pl.when(g == 0)
    def _():
        for other in range(1, groups):
            total_copy(other).start()
        sens_ref[...] = acc_out[0:1, :]
        for other in range(1, groups):
            total_copy(other).wait_send()

    @pl.when(g > 0)
    def _():
        acc_copy(g - 1).wait_send()
        state_copy(g - 1).wait_send()

    def drain(m, _):
        @pl.when(d > 0)
        def _():
            halo_copy(m, 0, d - 1).wait_send()

        @pl.when(d < width - 1)
        def _():
            halo_copy(m, 1, d + 1).wait_send()

        return 0

    lax.fori_loop(0, sweeps, drain, 0)
    for n in range(steps):
        level_copy(n).wait()


def per_device(groups, width, *args):
    (source, terminal, jacobian, face_coef, cell_coef, neighbours, send_blocks,
     live_count, volume, shape_field, weights) = args
    steps, nb, comp, cells = source.shape
    nei = face_coef.shape[1]
    count = send_blocks.shape[2]
    sweeps = steps * ITERS
    f32 = jnp.float32
    hbm = pl.BlockSpec(memory_space=pl.ANY)
    smem = pl.BlockSpec(memory_space=pltpu.SMEM)
    vmem = pltpu.VMEM
    dma = pltpu.SemaphoreType.DMA
    block = (nb, comp, cells)
    adjoint, sens = pl.pallas_call(
        functools.partial(kernel, groups, width),
        out_shape=(
            jax.ShapeDtypeStruct(source.shape, f32),
            jax.ShapeDtypeStruct((1, nb), f32),
        ),
        in_specs=[hbm, hbm, hbm, hbm, hbm, smem, smem, smem, hbm, hbm, smem],
        out_specs=(hbm, pl.BlockSpec(memory_space=pltpu.VMEM)),
        scratch_shapes=[
            vmem(source.shape, f32),
            vmem(block, f32),
            vmem(jacobian.shape[1:], f32),
            vmem(face_coef.shape, f32),
            vmem(cell_coef.shape, f32),
            vmem(volume.shape, f32),
            vmem(block, f32),
            vmem((nb + 1, comp, cells), f32),
            vmem(block, f32),
            vmem(block, f32),
            vmem(block, f32),
            vmem(block, f32),
            vmem(block, f32),
            vmem(source.shape, f32),
            vmem(block, f32),
            vmem((sweeps, 2 * count, comp, cells), f32),
            vmem((2 * count + 2, comp, cells), f32),
            vmem((sweeps, 2, count, comp, cells), f32),
            vmem((8, nb), f32),
            vmem((8, nb), f32),
            vmem((8, nb), f32),
            dma((7,)),
            dma((steps,)),
            dma((sweeps, 2)),
            dma((sweeps, 2)),
            dma,
            dma,
            dma,
            dma,
            dma((groups,)),
            dma,
        ],
        compiler_params=pltpu.CompilerParams(collective_id=0, has_side_effects=True),
    )(*args)
    return adjoint, sens.reshape(nb)


def solution(mesh):
    sizes = dict(mesh.shape)
    return jax.shard_map(
        functools.partial(per_device, sizes["tm"], sizes["space"]),
        mesh=mesh,
        in_specs=(
            P("tm", "space", None, None),
            P("space", None, None),
            P("tm", "space", None, None, None),
            P("space", None, None),
            P("space", None),
            P("space", None),
            P("space", None, None),
            P("space"),
            P("space", None),
            P("space", None, None),
            P("tm"),
        ),
        out_specs=(P("tm", "space", None, None), P("space")),
        check_vma=False,
    )
```

time: 564 us -> 143 us (0.25)
  local copies, waits for them, and re-layouts: 192 us -> 14.7 us
  other arithmetic: 170 us -> 0 us
  Pallas kernels: 0 us -> 126 us
  starting transfers between devices: 123 us -> 0 us
  waiting for transfers between devices: 60 us -> 0 us
  blocking collectives: 9.11 us -> 0 us
    gather x72 -> x0, local copies, waits for them, and re-layouts: 158 us -> none  [the longest x24 88 us: operate(): gathered = extended[neighbours]]
    pallas_call x0 -> x1, Pallas kernels: none -> 126 us  [per_device(): pl.pallas_call(functools.partial(kernel, groups, width), out_shape=(jax.S...]
    ppermute x51 -> x0, starting transfers between devices: 123 us -> none  [from_behind(): lax.ppermute(value, axis, [(source, source + steps) for source in range(f...]
    dot_general x48 -> x0, other arithmetic: 115 us -> none  [the longest x24 66.7 us: operate(): jnp.einsum('bnc,bnkc->bkc', face_coef, gathered, precision=highest)]
    ppermute x51 -> x0, waiting for transfers between devices: 60 us -> none  [from_behind(): lax.ppermute(value, axis, [(source, source + steps) for source in range(f...]
    mul x26 -> x0, other arithmetic: 26.5 us -> none  [the longest x24 25.3 us: level_step(): field = live * (field + precond * (rhs - operate(field, jac)))]
    while x372 -> x0, local copies, waits for them, and re-layouts: 20.5 us -> none
    concatenate x24 -> x0, other arithmetic: 17.3 us -> none  [operate(): extended = jnp.concatenate([field, from_lower, from_higher, blank], axis=0)]
  transfers between devices with their start and end apart: 51 -> 0, of which waited for: 19 -> 0; matrix products, arithmetic and copies ran while one was open for 14% -> 0% of each run, Pallas kernels for 0% -> 0%
where the time goes in v1:
time: 143 us; the launch traced here: 142 us
  Pallas kernels  126 us (88%)
  local copies, waits for them, and re-layouts  14.7 us (10%)
  between operations  1.45 us (1%)
    pallas_call x1, Pallas kernels, per_device(): pl.pallas_call(functools.partial(kernel, groups, width), out_shape=(jax.S...  126 us
    unnamed x12, local copies, waits for them, and re-layouts  14.7 us

profile of v1, /device:TPU:1, one launch (start us, length us, event | category | flops | bytes accessed | tf_op | source)
XLA Modules:
  0.0 142.1 jit_solution(1768524600355615446)
XLA Ops:
  0.6 0.0 copy-start
  0.6 0.0 copy-start.1
  1.4 1.4 %copy.17.nbr = s32[128,6]{1,0:T(8,128)} copy(s32[128,6]{0,1:T(8,128)} %param.16) | data formatting | bytes 6144 | tf_op args[5]
  2.9 2.0 %copy.14.terminal_hbm = f32[128,5,128]{2,1,0:T(8,128)} copy(f32[128,5,128]{2,0,1:T(8,128)} %param.12) | data formatting | bytes 655360 | tf_op args[1]
  4.8 2.1 %copy.16.face_hbm = f32[128,6,128]{2,1,0:T(8,128)} copy(f32[128,6,128]{2,0,1:T(8,128)} %param.14) | data formatting | bytes 786432 | tf_op args[3]
  6.9 2.0 %copy.18.shape_hbm = f32[128,5,128]{2,1,0:T(8,128)} copy(f32[128,5,128]{2,0,1:T(8,128)} %param.20) | data formatting | bytes 655360 | tf_op args[9]
  8.9 0.0 copy-done.1
  8.9 1.4 copy.13.source_hbm
  10.3 0.0 copy-done
  10.3 2.5 %copy.15.jac_hbm = f32[1,128,5,5,128]{4,3,2,1,0:T(8,128)} copy(f32[1,128,5,5,128]{4,1,3,2,0:T(8,128)S(1)} %copy-done) | data formatting | bytes 3276800 | tf_op args[2]
  12.8 126.0 %shard_map.122 = (f32[2,128,5,128]{3,2,1,0:T(8,128)}, f32[1,128]{1,0:T(1,128)}) custom-call(f32[2,128,5,128]{3,2,1,0:T(8,128)} %copy.13.source_hbm, f32[128,5,128]{2,1,0:T(8,128)} %copy.14.terminal_hbm, f32[1,128,5,5,128]{4,3,2,1,0:T(8,128)} %copy.15.jac_hbm, f32[128,6,128]{2,1,0:T(8,128)} %copy.16.face_hbm, f32[128,128]{1,0:T(8,128)} %cell_hbm.1, ...), custom_call_target="tpu_custom_call" | custom-call | tf_op jit(solution)/shard_map/pallas_call | solution.py:356
  138.8 2.2 %copy.19 = f32[2,128,5,128]{3,1,2,0:T(8,128)} copy(f32[2,128,5,128]{3,2,1,0:T(8,128)} %get-tuple-element.6) | data formatting | bytes 1310720
  141.0 1.1 copy.22
Async XLA Ops:
  0.6 9.7 %copy-start = (f32[1,128,5,5,128]{4,1,3,2,0:T(8,128)S(1)}, f32[1,128,5,5,128]{4,1,3,2,0:T(8,128)}, u32[]{:S(2)}) copy-start(f32[1,128,5,5,128]{4,1,3,2,0:T(8,128)} %param.13) | copy-start | bytes 4915204
  0.6 8.3 %copy-start.1 = (f32[2,128,5,128]{3,1,2,0:T(8,128)S(1)}, f32[2,128,5,128]{3,1,2,0:T(8,128)}, u32[]{:S(2)}) copy-start(f32[2,128,5,128]{3,1,2,0:T(8,128)} %param.11) | copy-start | bytes 1966084

commit v2 on v1

v2 whole, which is shorter than its diff:
```python
import functools

import jax
import jax.numpy as jnp
from jax import lax
from jax.experimental import pallas as pl
from jax.experimental.pallas import tpu as pltpu
from jax.sharding import PartitionSpec as P

ITERS = 3
INVERSE_STEP = 6.0
TILE = 16
HIGHEST = lax.Precision.HIGHEST


def split(x):
    high = x.astype(jnp.bfloat16)
    return high, (x - high.astype(jnp.float32)).astype(jnp.bfloat16)


def matmul(a, b, precision=None):
    return jnp.dot(a, b, precision=precision, preferred_element_type=jnp.float32)


def kernel(
    groups,
    width,
    source_hbm,
    terminal_hbm,
    jac_hbm,
    face_hbm,
    cell_hbm,
    nbr_hbm,
    send_blocks,
    live_count,
    volume_hbm,
    shape_hbm,
    weights,
    adjoint_hbm,
    sens_ref,
    source,
    terminal,
    jac,
    face,
    cell,
    nbr,
    volume,
    shape,
    field,
    part,
    rate,
    rate_mass,
    cell_left,
    cell_right,
    rhs,
    levels,
    weighted,
    near_pick,
    far_pick,
    field_terms,
    part_terms,
    halo_terms,
    near,
    far,
    select,
    select_terms,
    edge_pick,
    edge_face,
    edge_rate,
    edge_part,
    halo,
    outbox,
    acc_in,
    acc_out,
    total,
    load_sem,
    store_sem,
    halo_send,
    halo_recv,
    state_send,
    state_recv,
    acc_send,
    acc_recv,
    total_send,
    total_recv,
):
    g = lax.axis_index("tm")
    d = lax.axis_index("space")
    steps, comp, nb, cells = source.shape
    nei = face.shape[0]
    count = outbox.shape[3]
    sweeps = steps * ITERS
    tiles = nb // TILE
    edges = 2 * count

    loads = [
        pltpu.make_async_copy(nbr_hbm, nbr, load_sem.at[0]),
        pltpu.make_async_copy(face_hbm, face, load_sem.at[1]),
        pltpu.make_async_copy(cell_hbm, cell, load_sem.at[2]),
        pltpu.make_async_copy(volume_hbm, volume, load_sem.at[3]),
        pltpu.make_async_copy(jac_hbm.at[0], jac, load_sem.at[4]),
        pltpu.make_async_copy(terminal_hbm, terminal, load_sem.at[5]),
        pltpu.make_async_copy(source_hbm, source, load_sem.at[6]),
        pltpu.make_async_copy(shape_hbm, shape, load_sem.at[7]),
    ]
    for load in loads:
        load.start()

    @pl.when((d == 0) | (d == width - 1))
    def _():
        halo[...] = jnp.zeros_like(halo)

    barrier = pltpu.get_barrier_semaphore()
    for other in range(groups):
        @pl.when(g != other)
        def _():
            pl.semaphore_signal(barrier, inc=1, device_id={"tm": other})

    @pl.when(d > 0)
    def _():
        pl.semaphore_signal(barrier, inc=1, device_id={"space": d - 1})

    @pl.when(d < width - 1)
    def _():
        pl.semaphore_signal(barrier, inc=1, device_id={"space": d + 1})

    halo_terms[...] = jnp.zeros_like(halo_terms)
    lane = lax.broadcasted_iota(jnp.int32, (1, nb), 1)
    for side in range(2):
        for s in range(count):
            row = side * count + s
            select[pl.ds(row, 1), :] = jnp.where(lane == send_blocks[0, side, s], 1.0, 0.0)
    chosen = select[...]
    chosen_low = chosen.astype(jnp.bfloat16)
    select_terms[:, :nb] = chosen_low
    select_terms[:, nb:] = chosen_low

    loads[0].wait()
    listed = nbr[...].astype(jnp.float32)
    listed = jnp.concatenate([listed, jnp.zeros((nb - nei, nb), jnp.float32)], axis=0).T
    wide = lax.broadcasted_iota(jnp.int32, (nb, nb), 1).astype(jnp.float32)
    for k in range(nei):
        column = jnp.broadcast_to(listed[:, k : k + 1], (nb, nb))
        pick = jnp.where(column == wide, 1.0, 0.0).astype(jnp.bfloat16)
        near_pick[pl.ds(k * nb, nb), :nb] = pick
        near_pick[pl.ds(k * nb, nb), nb:] = pick
        outer = column - nb
        hit = (outer == wide) | (outer + edges == wide)
        inside = (outer >= 0) & (outer < edges)
        pick = jnp.where(hit & inside, 1.0, 0.0).astype(jnp.bfloat16)
        far_pick[pl.ds(k * nb, nb), :] = pick
        edge_pick[pl.ds(k * edges, edges), :] = matmul(chosen_low, pick).astype(jnp.bfloat16)

    for load in loads[1:5]:
        load.wait()
    alive = live_count[0]
    row_id = lax.broadcasted_iota(jnp.int32, (TILE, cells), 0)
    lane_id = lax.broadcasted_iota(jnp.int32, (TILE, cells), 1)

    def live_of(t):
        return jnp.where(row_id + t * TILE < alive, 1.0, 0.0)

    def prepare(t, _):
        r = pl.ds(pl.multiple_of(t * TILE, TILE), TILE)
        live = live_of(t)
        mass = INVERSE_STEP * volume[r, :]
        along = cell[r, :]
        base = mass + 2.0 * along
        for k in range(nei):
            base = base + face[k, r, :]
        cell_left[r, :] = jnp.where(lane_id == 0, 0.0, along)
        cell_right[r, :] = jnp.where(lane_id == cells - 1, 0.0, along)
        for j in range(comp):
            c = live / (base + jac[j, j, r, :])
            rate[j, r, :] = c
            drift = c * mass
            rate_mass[j, r, :] = drift
            for i in range(comp):
                entry = -c * jac[i, j, r, :]
                jac[i, j, r, :] = entry + (live - drift) if i == j else entry
            weighted[j, r, :] = jnp.zeros((TILE, cells), jnp.float32)
        return 0

    lax.fori_loop(0, tiles, prepare, 0)
    for k in range(nei):
        edge_face[k] = matmul(chosen, face[k], HIGHEST)
    for j in range(comp):
        edge_rate[j] = matmul(chosen, rate[j], HIGHEST)

    for load in loads[5:]:
        load.wait()
    pl.semaphore_wait(
        barrier,
        groups - 1 + jnp.where(d > 0, 1, 0) + jnp.where(d < width - 1, 1, 0),
    )

    def lanes(j):
        return slice(j * cells, (j + 1) * cells)

    def put_terms(ref, t, j, x):
        high, low = split(x)
        ref[pl.ds(pl.multiple_of(t * TILE, TILE), TILE), lanes(j)] = high
        ref[pl.ds(pl.multiple_of(nb + t * TILE, TILE), TILE), lanes(j)] = low

    def state_copy(to):
        return pltpu.make_async_remote_copy(
            src_ref=field, dst_ref=field, send_sem=state_send, recv_sem=state_recv,
            device_id={"tm": to},
        )

    @pl.when(g == groups - 1)
    def _():
        def begin(t, _):
            r = pl.ds(pl.multiple_of(t * TILE, TILE), TILE)
            for j in range(comp):
                field[j, r, :] = live_of(t) * terminal[j, r, :]
            return 0

        lax.fori_loop(0, tiles, begin, 0)

    @pl.when(g < groups - 1)
    def _():
        state_copy(g).wait_recv()

    def begin_terms(t, _):
        r = pl.ds(pl.multiple_of(t * TILE, TILE), TILE)
        for j in range(comp):
            put_terms(field_terms, t, j, field[j, r, :])
        return 0

    lax.fori_loop(0, tiles, begin_terms, 0)

    def halo_copy(m, side, to):
        return pltpu.make_async_remote_copy(
            src_ref=outbox.at[m, side],
            dst_ref=halo.at[m, 1 - side],
            send_sem=halo_send.at[m, side],
            recv_sem=halo_recv.at[m, 1 - side],
            device_id={"space": to},
        )

    def send(m):
        @pl.when(d > 0)
        def _():
            halo_copy(m, 0, d - 1).start()

        @pl.when(d < width - 1)
        def _():
            halo_copy(m, 1, d + 1).start()

    def receive(m):
        @pl.when(d > 0)
        def _():
            halo_copy(m, 1, d - 1).wait_recv()

        @pl.when(d < width - 1)
        def _():
            halo_copy(m, 0, d + 1).wait_recv()

    first_out = matmul(select_terms[...], field_terms[...])
    for side in range(2):
        for j in range(comp):
            outbox[0, side, j] = first_out[side * count : (side + 1) * count, lanes(j)]
    send(0)

    def sweep(m):
        near[...] = matmul(near_pick[...], field_terms[...])

        def local(t, _):
            r = pl.ds(pl.multiple_of(t * TILE, TILE), TILE)
            x = [field[i, r, :] for i in range(comp)]
            left = cell_left[r, :]
            right = cell_right[r, :]
            for j in range(comp):
                value = left * pltpu.roll(x[j], 1, 1) + right * pltpu.roll(x[j], cells - 1, 1)
                for k in range(nei):
                    q = pl.ds(pl.multiple_of(k * nb + t * TILE, TILE), TILE)
                    value = value + face[k, r, :] * near[q, lanes(j)]
                value = rhs[j, r, :] + rate[j, r, :] * value
                for i in range(comp):
                    value = value + jac[i, j, r, :] * x[i]
                part[j, r, :] = value
                put_terms(part_terms, t, j, value)
            return 0

        lax.fori_loop(0, tiles, local, 0)
        edge_part[...] = matmul(select_terms[...], part_terms[...])
        receive(m)
        for side in range(2):
            for j in range(comp):
                high, low = split(halo[m, side, j])
                halo_terms[side * count : (side + 1) * count, lanes(j)] = high
                halo_terms[edges + side * count : edges + (side + 1) * count, lanes(j)] = low

        @pl.when(m + 1 < sweeps)
        def _():
            arrived = matmul(edge_pick[...], halo_terms[...])
            for side in range(2):
                rows = slice(side * count, (side + 1) * count)
                for j in range(comp):
                    value = None
                    for k in range(nei):
                        q = slice(k * edges + side * count, k * edges + (side + 1) * count)
                        term = edge_face[k, rows, :] * arrived[q, lanes(j)]
                        value = term if value is None else value + term
                    outbox[m + 1, side, j] = edge_part[rows, lanes(j)] + edge_rate[j, rows, :] * value
            send(m + 1)

        far[...] = matmul(far_pick[...], halo_terms[...])

        def bulk(t, _):
            r = pl.ds(pl.multiple_of(t * TILE, TILE), TILE)
            for j in range(comp):
                value = None
                for k in range(nei):
                    q = pl.ds(pl.multiple_of(k * nb + t * TILE, TILE), TILE)
                    term = face[k, r, :] * far[q, lanes(j)]
                    value = term if value is None else value + term
                value = part[j, r, :] + rate[j, r, :] * value
                field[j, r, :] = value
                put_terms(field_terms, t, j, value)
            return 0

        lax.fori_loop(0, tiles, bulk, 0)

    def level_copy(n):
        return pltpu.make_async_copy(levels.at[n], adjoint_hbm.at[n], store_sem.at[n])

    def level(step, _):
        n = steps - 1 - step

        def start(t, _):
            r = pl.ds(pl.multiple_of(t * TILE, TILE), TILE)
            for j in range(comp):
                rhs[j, r, :] = rate[j, r, :] * source[n, j, r, :] + rate_mass[j, r, :] * field[j, r, :]
            return 0

        lax.fori_loop(0, tiles, start, 0)

        def inner(it, _):
            sweep(step * ITERS + it)
            return 0

        lax.fori_loop(0, ITERS, inner, 0)

        @pl.when((step == steps - 1) & (g > 0))
        def _():
            state_copy(g - 1).start()

        weight = weights[n]

        def finish(t, _):
            r = pl.ds(pl.multiple_of(t * TILE, TILE), TILE)
            for j in range(comp):
                x = field[j, r, :]
                levels[n, j, r, :] = x
                weighted[j, r, :] = weighted[j, r, :] + weight * x
            return 0

        lax.fori_loop(0, tiles, finish, 0)
        level_copy(n).start()
        return 0

    lax.fori_loop(0, steps, level, 0)

    summed = jnp.zeros((nb, cells), jnp.float32)
    for j in range(comp):
        summed = summed + weighted[j] * shape[j]

    mine = lax.dot_general(
        jnp.ones((8, cells), jnp.float32),
        summed,
        (((1,), (1,)), ((), ())),
        precision=lax.Precision.HIGHEST,
        preferred_element_type=jnp.float32,
    )

    def acc_copy(to):
        return pltpu.make_async_remote_copy(
            src_ref=acc_out, dst_ref=acc_in, send_sem=acc_send, recv_sem=acc_recv,
            device_id={"tm": to},
        )

    def total_copy(to):
        return pltpu.make_async_remote_copy(
            src_ref=acc_out, dst_ref=total, send_sem=total_send.at[to], recv_sem=total_recv,
            device_id={"tm": to},
        )

    @pl.when(g == groups - 1)
    def _():
        acc_out[...] = mine

    @pl.when(g < groups - 1)
    def _():
        acc_copy(g).wait_recv()
        acc_out[...] = mine + acc_in[...]

    @pl.when(g > 0)
    def _():
        acc_copy(g - 1).start()
        total_copy(g).wait_recv()
        sens_ref[...] = total[0:1, :]

    @pl.when(g == 0)
    def _():
        for other in range(1, groups):
            total_copy(other).start()
        sens_ref[...] = acc_out[0:1, :]
        for other in range(1, groups):
            total_copy(other).wait_send()

    @pl.when(g > 0)
    def _():
        acc_copy(g - 1).wait_send()
        state_copy(g - 1).wait_send()

    def drain(m, _):
        @pl.when(d > 0)
        def _():
            halo_copy(m, 0, d - 1).wait_send()

        @pl.when(d < width - 1)
        def _():
            halo_copy(m, 1, d + 1).wait_send()

        return 0

    lax.fori_loop(0, sweeps, drain, 0)
    for n in range(steps):
        level_copy(n).wait()


def per_device(groups, width, *args):
    (source, terminal, jacobian, face_coef, cell_coef, neighbours, send_blocks,
     live_count, volume, shape_field, weights) = args
    steps, nb, comp, cells = source.shape
    nei = face_coef.shape[1]
    count = send_blocks.shape[2]
    edges = 2 * count
    sweeps = steps * ITERS
    f32 = jnp.float32
    bf16 = jnp.bfloat16
    hbm = pl.BlockSpec(memory_space=pltpu.MemorySpace.HBM)
    smem = pl.BlockSpec(memory_space=pltpu.SMEM)
    vmem = pltpu.VMEM
    dma = pltpu.SemaphoreType.DMA
    block = (comp, nb, cells)
    flat = comp * cells
    adjoint, sens = pl.pallas_call(
        functools.partial(kernel, groups, width),
        out_shape=(
            jax.ShapeDtypeStruct((steps, comp, nb, cells), f32),
            jax.ShapeDtypeStruct((1, nb), f32),
        ),
        in_specs=[hbm, hbm, hbm, hbm, hbm, hbm, smem, smem, hbm, hbm, smem],
        out_specs=(hbm, pl.BlockSpec(memory_space=pltpu.VMEM)),
        scratch_shapes=[
            vmem((steps, comp, nb, cells), f32),
            vmem(block, f32),
            vmem((comp, comp, nb, cells), f32),
            vmem((nei, nb, cells), f32),
            vmem((nb, cells), f32),
            vmem((nei, nb), jnp.int32),
            vmem((nb, cells), f32),
            vmem(block, f32),
            vmem(block, f32),
            vmem(block, f32),
            vmem(block, f32),
            vmem(block, f32),
            vmem((nb, cells), f32),
            vmem((nb, cells), f32),
            vmem(block, f32),
            vmem((steps, comp, nb, cells), f32),
            vmem(block, f32),
            vmem((nei * nb, 2 * nb), bf16),
            vmem((nei * nb, nb), bf16),
            vmem((2 * nb, flat), bf16),
            vmem((2 * nb, flat), bf16),
            vmem((nb, flat), bf16),
            vmem((nei * nb, flat), f32),
            vmem((nei * nb, flat), f32),
            vmem((edges, nb), f32),
            vmem((edges, 2 * nb), bf16),
            vmem((nei * edges, nb), bf16),
            vmem((nei, edges, cells), f32),
            vmem((comp, edges, cells), f32),
            vmem((edges, flat), f32),
            vmem((sweeps, 2, comp, count, cells), f32),
            vmem((sweeps, 2, comp, count, cells), f32),
            vmem((8, nb), f32),
            vmem((8, nb), f32),
            vmem((8, nb), f32),
            dma((8,)),
            dma((steps,)),
            dma((sweeps, 2)),
            dma((sweeps, 2)),
            dma,
            dma,
            dma,
            dma,
            dma((groups,)),
            dma,
        ],
        compiler_params=pltpu.CompilerParams(collective_id=0, has_side_effects=True),
    )(
        source.transpose(0, 2, 1, 3),
        terminal.transpose(1, 0, 2),
        jacobian.transpose(0, 2, 3, 1, 4),
        face_coef.transpose(1, 0, 2),
        cell_coef,
        neighbours.T,
        send_blocks,
        live_count,
        volume,
        shape_field.transpose(1, 0, 2),
        weights,
    )
    return adjoint.transpose(0, 2, 1, 3), sens.reshape(nb)


def solution(mesh):
    sizes = dict(mesh.shape)
    return jax.shard_map(
        functools.partial(per_device, sizes["tm"], sizes["space"]),
        mesh=mesh,
        in_specs=(
            P("tm", "space", None, None),
            P("space", None, None),
            P("tm", "space", None, None, None),
            P("space", None, None),
            P("space", None),
            P("space", None),
            P("space", None, None),
            P("space"),
            P("space", None),
            P("space", None, None),
            P("tm"),
        ),
        out_specs=(P("tm", "space", None, None), P("space")),
        check_vma=False,
    )
```

time: 143 us -> 112 us (0.78)
  Pallas kernels: 126 us -> 107 us
  local copies, waits for them, and re-layouts: 14.7 us -> 3.14 us
    pallas_call x1, Pallas kernels: 126 us -> 107 us  [per_device(): pl.pallas_call(functools.partial(kernel, groups, width), out_shape=(jax.S...]
    unnamed x12 -> x2, local copies, waits for them, and re-layouts: 14.7 us -> 3.14 us
where the time goes in v2:
time: 112 us
  Pallas kernels  107 us (96%)
  local copies, waits for them, and re-layouts  3.14 us (3%)
  between operations  1.29 us (1%)
    pallas_call x1, Pallas kernels, per_device(): pl.pallas_call(functools.partial(kernel, groups, width), out_shape=(jax.S...  107 us
    unnamed x2, local copies, waits for them, and re-layouts  3.14 us

profile of v2, /device:TPU:1, one launch (start us, length us, event | category | flops | bytes accessed | tf_op | source)
XLA Modules:
  0.0 111.5 jit_solution(3416936328978538491)
XLA Ops:
  1.3 107.1 %shard_map.122 = (f32[2,5,128,128]{3,2,1,0:T(8,128)}, f32[1,128]{1,0:T(1,128)}) custom-call(f32[2,5,128,128]{3,2,1,0:T(8,128)} %bitcast.10, f32[5,128,128]{2,1,0:T(8,128)} %bitcast.12, f32[1,5,5,128,128]{4,3,2,1,0:T(8,128)} %bitcast.8, f32[6,128,128]{2,1,0:T(8,128)} %bitcast.11, f32[128,128]{1,0:T(8,128)} %cell_hbm.1, s32[6,128]{1,0:T(8,128)} %bitcast.14, ...), custom_call_target="tpu_custom_call" | custom-call | tf_op jit(solution)/shard_map/pallas_call | solution.py:450
  108.4 2.0 %copy.16 = f32[2,128,5,128]{3,1,2,0:T(8,128)} copy(f32[2,128,5,128]{3,1,2,0:T(8,128)} %bitcast.9) | data formatting | bytes 1310720
  110.4 1.2 %copy.17 = f32[128]{0:T(128)} copy(f32[128]{0:T(128)} %bitcast.15) | data formatting | bytes 1024

commit v3 on v2

--- a/solution.py
+++ b/solution.py
@@ -11,6 +11,10 @@
 INVERSE_STEP = 6.0
 TILE = 16
 HIGHEST = lax.Precision.HIGHEST
+
+
+def rows_at(start):
+    return pl.ds(start if isinstance(start, int) else pl.multiple_of(start, TILE), TILE)
 
 
 def split(x):
@@ -161,7 +165,7 @@
         return jnp.where(row_id + t * TILE < alive, 1.0, 0.0)
 
     def prepare(t, _):
-        r = pl.ds(pl.multiple_of(t * TILE, TILE), TILE)
+        r = rows_at(t * TILE)
         live = live_of(t)
         mass = INVERSE_STEP * volume[r, :]
         along = cell[r, :]
@@ -199,8 +203,8 @@
 
     def put_terms(ref, t, j, x):
         high, low = split(x)
-        ref[pl.ds(pl.multiple_of(t * TILE, TILE), TILE), lanes(j)] = high
-        ref[pl.ds(pl.multiple_of(nb + t * TILE, TILE), TILE), lanes(j)] = low
+        ref[rows_at(t * TILE), lanes(j)] = high
+        ref[rows_at(nb + t * TILE), lanes(j)] = low
 
     def state_copy(to):
         return pltpu.make_async_remote_copy(
@@ -211,7 +215,7 @@
     @pl.when(g == groups - 1)
     def _():
         def begin(t, _):
-            r = pl.ds(pl.multiple_of(t * TILE, TILE), TILE)
+            r = rows_at(t * TILE)
             for j in range(comp):
                 field[j, r, :] = live_of(t) * terminal[j, r, :]
             return 0
@@ -223,7 +227,7 @@
         state_copy(g).wait_recv()
 
     def begin_terms(t, _):
-        r = pl.ds(pl.multiple_of(t * TILE, TILE), TILE)
+        r = rows_at(t * TILE)
         for j in range(comp):
             put_terms(field_terms, t, j, field[j, r, :])
         return 0
@@ -267,14 +271,14 @@
         near[...] = matmul(near_pick[...], field_terms[...])
 
         def local(t, _):
-            r = pl.ds(pl.multiple_of(t * TILE, TILE), TILE)
+            r = rows_at(t * TILE)
             x = [field[i, r, :] for i in range(comp)]
             left = cell_left[r, :]
             right = cell_right[r, :]
             for j in range(comp):
                 value = left * pltpu.roll(x[j], 1, 1) + right * pltpu.roll(x[j], cells - 1, 1)
                 for k in range(nei):
-                    q = pl.ds(pl.multiple_of(k * nb + t * TILE, TILE), TILE)
+                    q = rows_at(k * nb + t * TILE)
                     value = value + face[k, r, :] * near[q, lanes(j)]
                 value = rhs[j, r, :] + rate[j, r, :] * value
                 for i in range(comp):
@@ -283,7 +287,8 @@
                 put_terms(part_terms, t, j, value)
             return 0
 
-        lax.fori_loop(0, tiles, local, 0)
+        for t in range(tiles):
+            local(t, 0)
         edge_part[...] = matmul(select_terms[...], part_terms[...])
         receive(m)
         for side in range(2):
@@ -309,11 +314,11 @@
         far[...] = matmul(far_pick[...], halo_terms[...])
 
         def bulk(t, _):
-            r = pl.ds(pl.multiple_of(t * TILE, TILE), TILE)
+            r = rows_at(t * TILE)
             for j in range(comp):
                 value = None
                 for k in range(nei):
-                    q = pl.ds(pl.multiple_of(k * nb + t * TILE, TILE), TILE)
+                    q = rows_at(k * nb + t * TILE)
                     term = face[k, r, :] * far[q, lanes(j)]
                     value = term if value is None else value + term
                 value = part[j, r, :] + rate[j, r, :] * value
@@ -321,7 +326,8 @@
                 put_terms(field_terms, t, j, value)
             return 0
 
-        lax.fori_loop(0, tiles, bulk, 0)
+        for t in range(tiles):
+            bulk(t, 0)
 
     def level_copy(n):
         return pltpu.make_async_copy(levels.at[n], adjoint_hbm.at[n], store_sem.at[n])
@@ -330,7 +336,7 @@
         n = steps - 1 - step
 
         def start(t, _):
-            r = pl.ds(pl.multiple_of(t * TILE, TILE), TILE)
+            r = rows_at(t * TILE)
             for j in range(comp):
                 rhs[j, r, :] = rate[j, r, :] * source[n, j, r, :] + rate_mass[j, r, :] * field[j, r, :]
             return 0
@@ -350,7 +356,7 @@
         weight = weights[n]
 
         def finish(t, _):
-            r = pl.ds(pl.multiple_of(t * TILE, TILE), TILE)
+            r = rows_at(t * TILE)
             for j in range(comp):
                 x = field[j, r, :]
                 levels[n, j, r, :] = x

time: 112 us -> 109 us (0.973)
  Pallas kernels: 107 us -> 104 us
    pallas_call x1, Pallas kernels: 107 us -> 104 us  [per_device(): pl.pallas_call(functools.partial(kernel, groups, width), out_shape=(jax.S...]
where the time goes in v3:
time: 109 us; the launch traced here: 108 us
  Pallas kernels  104 us (95%)
  local copies, waits for them, and re-layouts  3.14 us (3%)
  between operations  1.29 us (1%)
    pallas_call x1, Pallas kernels, per_device(): pl.pallas_call(functools.partial(kernel, groups, width), out_shape=(jax.S...  104 us
    unnamed x2, local copies, waits for them, and re-layouts  3.14 us

profile of v3, /device:TPU:1, one launch (start us, length us, event | category | flops | bytes accessed | tf_op | source)
XLA Modules:
  0.0 108.3 jit_solution(368866470941213826)
XLA Ops:
  1.3 103.9 %shard_map.122 = (f32[2,5,128,128]{3,2,1,0:T(8,128)}, f32[1,128]{1,0:T(1,128)}) custom-call(f32[2,5,128,128]{3,2,1,0:T(8,128)} %bitcast.10, f32[5,128,128]{2,1,0:T(8,128)} %bitcast.12, f32[1,5,5,128,128]{4,3,2,1,0:T(8,128)} %bitcast.8, f32[6,128,128]{2,1,0:T(8,128)} %bitcast.11, f32[128,128]{1,0:T(8,128)} %cell_hbm.1, s32[6,128]{1,0:T(8,128)} %bitcast.14, ...), custom_call_target="tpu_custom_call" | custom-call | tf_op jit(solution)/shard_map/pallas_call | solution.py:456
  105.2 2.0 %copy.16 = f32[2,128,5,128]{3,1,2,0:T(8,128)} copy(f32[2,128,5,128]{3,1,2,0:T(8,128)} %bitcast.9) | data formatting | bytes 1310720
  107.2 1.2 %copy.17 = f32[128]{0:T(128)} copy(f32[128]{0:T(128)} %bitcast.15) | data formatting | bytes 1024

commit v4 on v3

--- a/solution.py
+++ b/solution.py
@@ -96,6 +96,7 @@
     sweeps = steps * ITERS
     tiles = nb // TILE
     edges = 2 * count
+    chunks = [(a, min(a + 2, comp)) for a in range(0, comp, 2)]
 
     loads = [
         pltpu.make_async_copy(nbr_hbm, nbr, load_sem.at[0]),
@@ -120,13 +121,24 @@
         def _():
             pl.semaphore_signal(barrier, inc=1, device_id={"tm": other})
 
+    def greet(side):
+        pl.semaphore_signal(barrier, inc=1, device_id={"space": side})
+
+        @pl.when(g > 0)
+        def _():
+            pl.semaphore_signal(barrier, inc=1, device_id={"tm": g - 1, "space": side})
+
+        @pl.when(g < groups - 1)
+        def _():
+            pl.semaphore_signal(barrier, inc=1, device_id={"tm": g + 1, "space": side})
+
     @pl.when(d > 0)
     def _():
-        pl.semaphore_signal(barrier, inc=1, device_id={"space": d - 1})
+        greet(d - 1)
 
     @pl.when(d < width - 1)
     def _():
-        pl.semaphore_signal(barrier, inc=1, device_id={"space": d + 1})
+        greet(d + 1)
 
     halo_terms[...] = jnp.zeros_like(halo_terms)
     lane = lax.broadcasted_iota(jnp.int32, (1, nb), 1)
@@ -193,10 +205,9 @@
 
     for load in loads[5:]:
         load.wait()
-    pl.semaphore_wait(
-        barrier,
-        groups - 1 + jnp.where(d > 0, 1, 0) + jnp.where(d < width - 1, 1, 0),
-    )
+    sides = jnp.where(d > 0, 1, 0) + jnp.where(d < width - 1, 1, 0)
+    slabs = 1 + jnp.where(g > 0, 1, 0) + jnp.where(g < groups - 1, 1, 0)
+    pl.semaphore_wait(barrier, groups - 1 + sides * slabs)
 
     def lanes(j):
         return slice(j * cells, (j + 1) * cells)
@@ -234,38 +245,47 @@
 
     lax.fori_loop(0, tiles, begin_terms, 0)
 
-    def halo_copy(m, side, to):
+    def halo_copy(slot, side, c, to):
+        own = slot < sweeps
+        first, last = chunks[c]
+        part_of = pl.ds(first, last - first)
+        place = jnp.where(own, slot, 0)
         return pltpu.make_async_remote_copy(
-            src_ref=outbox.at[m, side],
-            dst_ref=halo.at[m, 1 - side],
-            send_sem=halo_send.at[m, side],
-            recv_sem=halo_recv.at[m, 1 - side],
-            device_id={"space": to},
+            src_ref=outbox.at[slot, side, part_of],
+            dst_ref=halo.at[place, 1 - side, part_of],
+            send_sem=halo_send.at[slot, side, c],
+            recv_sem=halo_recv.at[place, 1 - side, c],
+            device_id={"tm": jnp.where(own, g, g - 1), "space": to},
         )
 
-    def send(m):
+    def send(slot, c):
+        wanted = (slot < sweeps) | (g > 0)
+
+        @pl.when((d > 0) & wanted)
+        def _():
+            halo_copy(slot, 0, c, d - 1).start()
+
+        @pl.when((d < width - 1) & wanted)
+        def _():
+            halo_copy(slot, 1, c, d + 1).start()
+
+    def receive(m, c):
         @pl.when(d > 0)
         def _():
-            halo_copy(m, 0, d - 1).start()
+            halo_copy(m, 1, c, d - 1).wait_recv()
 
         @pl.when(d < width - 1)
         def _():
-            halo_copy(m, 1, d + 1).start()
-
-    def receive(m):
-        @pl.when(d > 0)
-        def _():
-            halo_copy(m, 1, d - 1).wait_recv()
-
-        @pl.when(d < width - 1)
-        def _():
-            halo_copy(m, 0, d + 1).wait_recv()
-
-    first_out = matmul(select_terms[...], field_terms[...])
-    for side in range(2):
-        for j in range(comp):
-            outbox[0, side, j] = first_out[side * count : (side + 1) * count, lanes(j)]
-    send(0)
+            halo_copy(m, 0, c, d + 1).wait_recv()
+
+    @pl.when(g == groups - 1)
+    def _():
+        first_out = matmul(select_terms[...], field_terms[...])
+        for side in range(2):
+            for j in range(comp):
+                outbox[0, side, j] = first_out[side * count : (side + 1) * count, lanes(j)]
+        for c in range(len(chunks)):
+            send(0, c)
 
     def sweep(m):
         near[...] = matmul(near_pick[...], field_terms[...])
@@ -290,26 +310,25 @@
         for t in range(tiles):
             local(t, 0)
         edge_part[...] = matmul(select_terms[...], part_terms[...])
-        receive(m)
-        for side in range(2):
-            for j in range(comp):
-                high, low = split(halo[m, side, j])
-                halo_terms[side * count : (side + 1) * count, lanes(j)] = high
-                halo_terms[edges + side * count : edges + (side + 1) * count, lanes(j)] = low
-
-        @pl.when(m + 1 < sweeps)
-        def _():
-            arrived = matmul(edge_pick[...], halo_terms[...])
+        for c, (first, last) in enumerate(chunks):
+            receive(m, c)
+            for side in range(2):
+                low_rows = slice(edges + side * count, edges + (side + 1) * count)
+                for j in range(first, last):
+                    high, low = split(halo[m, side, j])
+                    halo_terms[side * count : (side + 1) * count, lanes(j)] = high
+                    halo_terms[low_rows, lanes(j)] = low
+            arrived = matmul(edge_pick[...], halo_terms[:, first * cells : last * cells])
             for side in range(2):
                 rows = slice(side * count, (side + 1) * count)
-                for j in range(comp):
+                for j in range(first, last):
                     value = None
                     for k in range(nei):
                         q = slice(k * edges + side * count, k * edges + (side + 1) * count)
-                        term = edge_face[k, rows, :] * arrived[q, lanes(j)]
+                        term = edge_face[k, rows, :] * arrived[q, lanes(j - first)]
                         value = term if value is None else value + term
                     outbox[m + 1, side, j] = edge_part[rows, lanes(j)] + edge_rate[j, rows, :] * value
-            send(m + 1)
+            send(m + 1, c)
 
         far[...] = matmul(far_pick[...], halo_terms[...])
 
@@ -421,18 +440,20 @@
         acc_copy(g - 1).wait_send()
         state_copy(g - 1).wait_send()
 
-    def drain(m, _):
-        @pl.when(d > 0)
-        def _():
-            halo_copy(m, 0, d - 1).wait_send()
-
-        @pl.when(d < width - 1)
-        def _():
-            halo_copy(m, 1, d + 1).wait_send()
+    def drain(slot, _):
+        wanted = ((slot > 0) | (g == groups - 1)) & ((slot < sweeps) | (g > 0))
+        for c in range(len(chunks)):
+            @pl.when((d > 0) & wanted)
+            def _():
+                halo_copy(slot, 0, c, d - 1).wait_send()
+
+            @pl.when((d < width - 1) & wanted)
+            def _():
+                halo_copy(slot, 1, c, d + 1).wait_send()
 
         return 0
 
-    lax.fori_loop(0, sweeps, drain, 0)
+    lax.fori_loop(0, sweeps + 1, drain, 0)
     for n in range(steps):
         level_copy(n).wait()
 
@@ -453,6 +474,7 @@
     dma = pltpu.SemaphoreType.DMA
     block = (comp, nb, cells)
     flat = comp * cells
+    chunks = -(-comp // 2)
     adjoint, sens = pl.pallas_call(
         functools.partial(kernel, groups, width),
         out_shape=(
@@ -493,14 +515,14 @@
             vmem((comp, edges, cells), f32),
             vmem((edges, flat), f32),
             vmem((sweeps, 2, comp, count, cells), f32),
-            vmem((sweeps, 2, comp, count, cells), f32),
+            vmem((sweeps + 1, 2, comp, count, cells), f32),
             vmem((8, nb), f32),
             vmem((8, nb), f32),
             vmem((8, nb), f32),
             dma((8,)),
             dma((steps,)),
-            dma((sweeps, 2)),
-            dma((sweeps, 2)),
+            dma((sweeps + 1, 2, chunks)),
+            dma((sweeps, 2, chunks)),
             dma,
             dma,
             dma,

time: 109 us -> 104 us (0.954)
  Pallas kernels: 104 us -> 98.9 us
    pallas_call x1, Pallas kernels: 104 us -> 98.9 us  [per_device(): pl.pallas_call(functools.partial(kernel, groups, width), out_shape=(jax.S...]
where the time goes in v4:
time: 104 us; the launch traced here: 103 us
  Pallas kernels  98.9 us (95%)
  local copies, waits for them, and re-layouts  3.14 us (3%)
  between operations  1.29 us (1%)
    pallas_call x1, Pallas kernels, per_device(): pl.pallas_call(functools.partial(kernel, groups, width), out_shape=(jax.S...  98.9 us
    unnamed x2, local copies, waits for them, and re-layouts  3.14 us

profile of v4, /device:TPU:1, one launch (start us, length us, event | category | flops | bytes accessed | tf_op | source)
XLA Modules:
  0.0 103.3 jit_solution(2341769581076230190)
XLA Ops:
  1.3 98.9 %shard_map.122 = (f32[2,5,128,128]{3,2,1,0:T(8,128)}, f32[1,128]{1,0:T(1,128)}) custom-call(f32[2,5,128,128]{3,2,1,0:T(8,128)} %bitcast.10, f32[5,128,128]{2,1,0:T(8,128)} %bitcast.12, f32[1,5,5,128,128]{4,3,2,1,0:T(8,128)} %bitcast.8, f32[6,128,128]{2,1,0:T(8,128)} %bitcast.11, f32[128,128]{1,0:T(8,128)} %cell_hbm.1, s32[6,128]{1,0:T(8,128)} %bitcast.14, ...), custom_call_target="tpu_custom_call" | custom-call | tf_op jit(solution)/shard_map/pallas_call | solution.py:478
  100.2 2.0 %copy.16 = f32[2,128,5,128]{3,1,2,0:T(8,128)} copy(f32[2,128,5,128]{3,1,2,0:T(8,128)} %bitcast.9) | data formatting | bytes 1310720
  102.2 1.2 %copy.17 = f32[128]{0:T(128)} copy(f32[128]{0:T(128)} %bitcast.15) | data formatting | bytes 1024

commit v5 on v4

--- a/solution.py
+++ b/solution.py
@@ -197,7 +197,8 @@
             weighted[j, r, :] = jnp.zeros((TILE, cells), jnp.float32)
         return 0
 
-    lax.fori_loop(0, tiles, prepare, 0)
+    for t in range(tiles):
+        prepare(t, 0)
     for k in range(nei):
         edge_face[k] = matmul(chosen, face[k], HIGHEST)
     for j in range(comp):
@@ -231,7 +232,8 @@
                 field[j, r, :] = live_of(t) * terminal[j, r, :]
             return 0
 
-        lax.fori_loop(0, tiles, begin, 0)
+        for t in range(tiles):
+            begin(t, 0)
 
     @pl.when(g < groups - 1)
     def _():
@@ -243,7 +245,8 @@
             put_terms(field_terms, t, j, field[j, r, :])
         return 0
 
-    lax.fori_loop(0, tiles, begin_terms, 0)
+    for t in range(tiles):
+        begin_terms(t, 0)
 
     def halo_copy(slot, side, c, to):
         own = slot < sweeps
@@ -360,7 +363,8 @@
                 rhs[j, r, :] = rate[j, r, :] * source[n, j, r, :] + rate_mass[j, r, :] * field[j, r, :]
             return 0
 
-        lax.fori_loop(0, tiles, start, 0)
+        for t in range(tiles):
+            start(t, 0)
 
         def inner(it, _):
             sweep(step * ITERS + it)
@@ -382,7 +386,8 @@
                 weighted[j, r, :] = weighted[j, r, :] + weight * x
             return 0
 
-        lax.fori_loop(0, tiles, finish, 0)
+        for t in range(tiles):
+            finish(t, 0)
         level_copy(n).start()
         return 0
 

time: 104 us -> 103 us (level)
  no operation moved by 1% of the time
where the time goes in v5:
time: 103 us; the launch traced here: 102 us
  Pallas kernels  98 us (95%)
  local copies, waits for them, and re-layouts  3.14 us (3%)
  between operations  1.29 us (1%)
    pallas_call x1, Pallas kernels, per_device(): pl.pallas_call(functools.partial(kernel, groups, width), out_shape=(jax.S...  98 us
    unnamed x2, local copies, waits for them, and re-layouts  3.14 us

profile of v5, /device:TPU:1, one launch (start us, length us, event | category | flops | bytes accessed | tf_op | source)
XLA Modules:
  0.0 102.4 jit_solution(6459686978901896086)
XLA Ops:
  1.3 98.0 %shard_map.122 = (f32[2,5,128,128]{3,2,1,0:T(8,128)}, f32[1,128]{1,0:T(1,128)}) custom-call(f32[2,5,128,128]{3,2,1,0:T(8,128)} %bitcast.10, f32[5,128,128]{2,1,0:T(8,128)} %bitcast.12, f32[1,5,5,128,128]{4,3,2,1,0:T(8,128)} %bitcast.8, f32[6,128,128]{2,1,0:T(8,128)} %bitcast.11, f32[128,128]{1,0:T(8,128)} %cell_hbm.1, s32[6,128]{1,0:T(8,128)} %bitcast.14, ...), custom_call_target="tpu_custom_call" | custom-call | tf_op jit(solution)/shard_map/pallas_call | solution.py:483
  99.2 2.0 %copy.16 = f32[2,128,5,128]{3,1,2,0:T(8,128)} copy(f32[2,128,5,128]{3,1,2,0:T(8,128)} %bitcast.9) | data formatting | bytes 1310720
  101.2 1.2 %copy.17 = f32[128]{0:T(128)} copy(f32[128]{0:T(128)} %bitcast.15) | data formatting | bytes 1024
